TPU v7x, 32 devices: a whole 2x2x4 slice. The times are simulated.
32 devices in a mesh: cfg: 2 (over y), ta: 4 (over z), sa: 2 (over x), src: 2 (over core).
Axes of the slice: x: 2, y: 2, z: 4, core: 2. Of those that a mesh axis runs over, the one named last changes fastest.
Arguments:
- prop: bfloat16 [4, 8, 2, 12, 12, 512], P(('cfg', 'src'), 'ta', None, None, None, 'sa'), parts along dimension 0, may hold values from -6 to 6
- eps_rows: int32 [24, 3], replicated, may hold values from 0 to 11
- eps_sign: int32 [24], replicated, may hold values from 0 to 1
- source_sites: int32 [4, 3], P('cfg'), parts along dimension 0, may hold values from 0 to 15, as said below
- momenta: int32 [8, 3], replicated, may hold values from -2 to 2
Outputs:
- blocks: float32 [4, 8, 2, 8, 1728], P('cfg', None, None, 'ta', 'sa'), parts along dimension 0
There are 2 independent parts, one for each index of `cfg`. A program takes and returns all parts, laid end to end along the dimension named above; an argument that names none is the same for every part. Nothing has to cross between parts.
Inputs may be any that keep to these rules, and one draw needn't show every extreme that they name: `source_sites`: each row is a lattice site: first coordinate below 2, second below 16, third below 16.
All inputs are finite; a program needn't handle non-finite values.
Results may differ from a plain program's by a relative error of at most 0.0045.
Values sent between devices are 32-bit elements; how exact they have to be, the bound alone decides.
A program may use at most 128 MiB of HBM per device.

v0:
```python
import math

import jax
import jax.numpy as jnp
from jax import lax
from jax.sharding import PartitionSpec as P

LY = 16
LZ = 16


def phase_table(position, momenta, site_index, extent_x):
    coord_x = site_index // (LY * LZ)
    coord_y = site_index // LZ % LY
    coord_z = site_index % LZ
    part_x = momenta[:, 0:1] * (coord_x[None, :] - position[0]) % extent_x
    part_y = momenta[:, 1:2] * (coord_y[None, :] - position[1]) % LY
    part_z = momenta[:, 2:3] * (coord_z[None, :] - position[2]) % LZ
    angle = (
        2.0
        * math.pi
        * (
            part_x.astype(jnp.float32) / extent_x
            + part_y.astype(jnp.float32) / LY
            + part_z.astype(jnp.float32) / LZ
        )
    )
    return jnp.concatenate([jnp.cos(angle), jnp.sin(angle)], axis=0).astype(jnp.bfloat16)


def contract(slab, rows, weights):
    first = jnp.take(slab, rows[:, 0], axis=1).astype(jnp.float32)
    second = jnp.take(slab, rows[:, 1], axis=1).astype(jnp.float32)
    third = jnp.take(slab, rows[:, 2], axis=1)
    scaled = weights[:, None, None, None]
    real = scaled * (
        first[0][:, :, None] * second[0][:, None] - first[1][:, :, None] * second[1][:, None]
    )
    imag = scaled * (
        first[0][:, :, None] * second[1][:, None] + first[1][:, :, None] * second[0][:, None]
    )
    pair = jnp.stack([real, imag]).astype(jnp.bfloat16)
    mixer = jnp.stack([jnp.stack([third[0], -third[1]]), jnp.stack([third[1], third[0]])])
    block = jnp.einsum("ceijx,oceLx->oijLx", pair, mixer, preferred_element_type=jnp.float32)
    width = slab.shape[1]
    return block.astype(jnp.bfloat16).reshape(2 * width * width * width, slab.shape[-1])


def mix_phase(table, quark):
    product = lax.dot_general(
        table, quark, (((1,), (1,)), ((), ())), preferred_element_type=jnp.float32
    )
    half_m = table.shape[0] // 2
    half_k = quark.shape[0] // 2
    cos_re = product[:half_m, :half_k]
    cos_im = product[:half_m, half_k:]
    sin_re = product[half_m:, :half_k]
    sin_im = product[half_m:, half_k:]
    return jnp.stack([cos_re + sin_im, cos_im - sin_re])


def per_device(prop, eps_rows, eps_sign, source_sites, momenta):
    src_count = prop.shape[0]
    time_count = prop.shape[1]
    width = prop.shape[3]
    site_count = prop.shape[5]
    sites_total = site_count * lax.axis_size("sa")
    extent_x = sites_total // (LY * LZ)
    site_index = lax.axis_index("sa") * site_count + jnp.arange(site_count, dtype=jnp.int32)
    weights = (2 * eps_sign - 1).astype(jnp.float32)
    scale = 1.0 / math.sqrt(4.0 * eps_rows.shape[0] * sites_total)
    first_source = lax.axis_index("src") * src_count
    positions = lax.dynamic_slice_in_dim(source_sites, first_source, src_count, 0)
    tables = jnp.stack([phase_table(positions[0], momenta, site_index, extent_x)])
    slabs = prop.reshape((src_count * time_count,) + prop.shape[2:])
    owners = jnp.repeat(jnp.arange(src_count, dtype=jnp.int32), time_count)

    def project(items):
        slab, owner = items
        quark = contract(slab, eps_rows, weights)
        return scale * mix_phase(tables[owner], quark)

    partial_value = lax.map(project, (slabs, owners))
    partial_value = partial_value.reshape(
        src_count, time_count, 2, momenta.shape[0], width * width * width
    )
    summed = lax.psum_scatter(partial_value, "sa", scatter_dimension=4, tiled=True)
    finished = lax.all_to_all(summed, "ta", split_axis=3, concat_axis=1, tiled=True)
    return lax.all_gather(finished, "src", axis=0, tiled=True)


def solution(mesh):
    return jax.shard_map(
        per_device,
        mesh=mesh,
        in_specs=(P(("cfg", "src"), "ta", None, None, None, "sa"), P(), P(), P("cfg", None), P()),
        out_specs=P("cfg", None, None, "ta", "sa"),
        check_vma=False,
    )
```

profile of v0, /device:TPU:0, one launch (start us, length us, event | category | flops | bytes accessed | tf_op | source)
XLA Modules:
  0.0 323.2 jit_solution(15552078244908661821)
XLA Ops:
  8.7 1.1 add_convert_fusion
  10.5 1.3 fusion.20
  11.9 257.3 %while.10 = (s32[]{:T(128)}, f32[2,2,8,1728]{3,2,1,0:T(8,128)}, bf16[2,2,12,12,256]{4,1,3,2,0:T(2,128)(2,1)}, s32[24,3]{0,1:T(4,128)}, f32[24]{0:T(128)}, /*index=5*/bf16[1,16,256]{2,1,0:T(8,128)(2,1)S(1)}, s32[]{:T(128)}) while((s32[]{:T(128)}, f32[2,2,8,1728]{3,2,1,0:T(8,128)}, bf16[2,2,12,12,256]{4,1,3,2,0:T(2,128)(2,1)}, ...), condition=%wide.region_1.3_spmd, body=%wide.region_0.2_spmd.sunk | while | flops 126235056 | bytes 50939416 | solution.py:83
  12.0 1.3 compare_and_fusion.4
  14.3 1.1 gather_fusion.1
  15.5 1.1 gather_fusion.2
  18.4 1.8 multiply_convert_fusion.3
  20.6 34.0 %copy.83 = bf16[2,24,12,12,256,1]{1,3,0,2,5,4:T(8,128)(2,1)} copy(bf16[2,24,12,12,256,1]{4,1,3,2,0,5:T(8,128)(2,1)S(1)} %maximum_bitcast_fusion.9) | data formatting | bytes 7077888 | tf_op jit(solution)/shard_map/while/body/eval_jaxpr/stack | solution.py:42
  54.6 2.0 gather_fusion
  58.7 6.5 %copy.78 = bf16[2,2,24,12,256,1]{2,3,1,5,0,4:T(8,128)(2,1)} copy(bf16[2,2,24,12,256,1]{4,2,3,1,0,5:T(8,128)(2,1)S(1)} %maximum_bitcast_fusion.8) | data formatting | bytes 1179648 | tf_op jit(solution)/shard_map/while/body/eval_jaxpr/stack | solution.py:43
  65.2 41.2 %fusion.48 = bf16[2,12,12,12,256]{2,3,1,0,4:T(8,128)(2,1)} fusion(bf16[2,2,24,12,256,1]{2,3,1,5,0,4:T(8,128)(2,1)} %copy.78, bf16[2,24,12,12,256,1]{1,3,0,2,5,4:T(8,128)(2,1)} %copy.83), kind=kOutput, calls=%fused_computation.4.clone.1 | convolution fusion | flops 85819392 | bytes 5898240 | tf_op jit(solution)/shard_map/while/body/eval_jaxpr/ceijx,oceLx->oijLx/dot_general | solution.py:44
  106.4 29.3 %copy.84 = bf16[2,12,12,12,256]{4,3,2,1,0:T(8,128)(2,1)S(1)} copy(bf16[2,12,12,12,256]{2,3,1,0,4:T(8,128)(2,1)} %fusion.48) | data formatting | bytes 3538944 | tf_op jit(solution)/shard_map/while/body/eval_jaxpr/convert_element_type | solution.py:46
  135.7 2.0 reshape.465
  137.7 2.0 convolution_bitcast_fusion.2
  140.6 1.3 compare_and_fusion.4
  142.9 1.1 gather_fusion.1
  144.1 1.1 gather_fusion.2
  147.1 1.8 multiply_convert_fusion.3
  149.2 34.0 %copy.83 = bf16[2,24,12,12,256,1]{1,3,0,2,5,4:T(8,128)(2,1)} copy(bf16[2,24,12,12,256,1]{4,1,3,2,0,5:T(8,128)(2,1)S(1)} %maximum_bitcast_fusion.9) | data formatting | bytes 7077888 | tf_op jit(solution)/shard_map/while/body/eval_jaxpr/stack | solution.py:42
  183.2 2.0 gather_fusion
  187.3 6.5 %copy.78 = bf16[2,2,24,12,256,1]{2,3,1,5,0,4:T(8,128)(2,1)} copy(bf16[2,2,24,12,256,1]{4,2,3,1,0,5:T(8,128)(2,1)S(1)} %maximum_bitcast_fusion.8) | data formatting | bytes 1179648 | tf_op jit(solution)/shard_map/while/body/eval_jaxpr/stack | solution.py:43
  193.8 41.2 %fusion.48 = bf16[2,12,12,12,256]{2,3,1,0,4:T(8,128)(2,1)} fusion(bf16[2,2,24,12,256,1]{2,3,1,5,0,4:T(8,128)(2,1)} %copy.78, bf16[2,24,12,12,256,1]{1,3,0,2,5,4:T(8,128)(2,1)} %copy.83), kind=kOutput, calls=%fused_computation.4.clone.1 | convolution fusion | flops 85819392 | bytes 5898240 | tf_op jit(solution)/shard_map/while/body/eval_jaxpr/ceijx,oceLx->oijLx/dot_general | solution.py:44
  235.0 29.3 %copy.84 = bf16[2,12,12,12,256]{4,3,2,1,0:T(8,128)(2,1)S(1)} copy(bf16[2,12,12,12,256]{2,3,1,0,4:T(8,128)(2,1)} %fusion.48) | data formatting | bytes 3538944 | tf_op jit(solution)/shard_map/while/body/eval_jaxpr/convert_element_type | solution.py:46
  264.3 2.0 reshape.465
  266.3 2.0 convolution_bitcast_fusion.2
  269.2 4.4 %copy.54 = f32[1,2,2,8,1728]{3,2,1,0,4:T(2,128)S(1)} copy(f32[1,2,2,8,1728]{4,3,2,1,0:T(8,128)} %bitcast.122) | data formatting | bytes 442368
  273.6 3.5 %reshape.450 = f32[1728,32]{1,0:T(8,128)} reshape(f32[1728,1,2,2,8]{4,3,2,1,0:T(2,128)S(1)} %bitcast.118) | data formatting | bytes 442368
  277.2 21.5 %reduce-scatter.4.cloned.1.call-done = f32[864,32]{1,0:T(8,128)} async-done(((f32[1728,32]{1,0:T(8,128)}), f32[864,32]{1,0:T(8,128)}) %reduce-scatter.4.cloned.1.call-update) | async-done | bytes 110608
  298.6 2.7 reshape.451
  301.3 1.8 copy.44
  303.2 10.3 %all_to_all.18 = f32[1,2,2,8,864]{4,2,1,0,3:T(2,128)S(1)} all-to-all(f32[1,2,2,8,864]{4,2,1,0,3:T(2,128)S(1)} %copy.44), channel_id=1, replica_groups=mesh['cfg'=2,'ta'=4,'sa'=2,'src'=2] {'ta'}, dimensions={3} | all-to-all | bytes 221184 | tf_op jit(solution)/shard_map/all_to_all | solution.py:88
  313.6 2.0 all_gather.3
  (70 shorter events, 15.7 us)
Async XLA Ops:
  6.5 0.7 copy-start
  6.5 292.1 %reduce-scatter.4.cloned.1.call-start = ((), (), s32[]{:S(2)}) async-start(), calls=%async_computation.2 | async-start | bytes 1327104
  14.3 4.1 %copy-start.2 = (bf16[2,12,12,256]{3,0,2,1:T(2,128)(2,1)}, bf16[2,12,12,256]{3,0,2,1:T(2,128)(2,1)S(1)}, u32[]{:S(2)}) copy-start(bf16[2,12,12,256]{3,0,2,1:T(2,128)(2,1)S(1)} %dynamic-slice_bitcast_fusion.2) | copy-start | bytes 442372 | tf_op jit(solution)/shard_map/while
  135.7 4.1 %copy-start.3 = (f32[2,2,8,1728]{3,2,1,0:T(8,128)S(1)}, f32[2,2,8,1728]{3,2,1,0:T(8,128)}, u32[]{:S(2)}) copy-start(f32[2,2,8,1728]{3,2,1,0:T(8,128)} %get-tuple-element.173) | copy-start | bytes 663556 | tf_op jit(solution)/shard_map/while
  139.9 0.7 copy-start.4
  142.9 4.1 %copy-start.2 = (bf16[2,12,12,256]{3,0,2,1:T(2,128)(2,1)}, bf16[2,12,12,256]{3,0,2,1:T(2,128)(2,1)S(1)}, u32[]{:S(2)}) copy-start(bf16[2,12,12,256]{3,0,2,1:T(2,128)(2,1)S(1)} %dynamic-slice_bitcast_fusion.2) | copy-start | bytes 442372 | tf_op jit(solution)/shard_map/while
  264.3 4.1 %copy-start.3 = (f32[2,2,8,1728]{3,2,1,0:T(8,128)S(1)}, f32[2,2,8,1728]{3,2,1,0:T(8,128)}, u32[]{:S(2)}) copy-start(f32[2,2,8,1728]{3,2,1,0:T(8,128)} %get-tuple-element.173) | copy-start | bytes 663556 | tf_op jit(solution)/shard_map/while
  268.5 0.7 copy-start.4
  273.6 42.8 %copy-start.1 = (s32[2,3]{1,0:T(2,128)S(1)}, s32[2,3]{1,0:T(2,128)}, u32[]{:S(2)}) copy-start(s32[2,3]{1,0:T(2,128)} %param.12) | copy-start | bytes 76
Sparse Core Ops, SparseCore 0:
  277.3 21.2 reduce-scatter.3
where the time goes:
time: 325 us; the launch traced here: 323 us
  local copies, waits for them, and re-layouts  174 us (54%)
  matrix products  86.5 us (27%)
  waiting for transfers between devices  21.5 us (7%)
  other arithmetic  15.3 us (5%)
  between operations  13.5 us (4%)
  blocking collectives  12.3 us (4%)
    dot_general x2, matrix products, contract(): jnp.einsum('ceijx,oceLx->oijLx', pair, mixer, preferred_element_type=jnp....  82.4 us
    another operation x2, local copies, waits for them, and re-layouts, contract(): pair = jnp.stack([real, imag]).astype(jnp.bfloat16)  68 us
    convert_element_type x2, local copies, waits for them, and re-layouts, contract(): block.astype(jnp.bfloat16)  58.5 us
    unnamed x2, waiting for transfers between devices  21.5 us
    another operation x2, local copies, waits for them, and re-layouts, contract(): jnp.stack([jnp.stack([third[0], -third[1]]), jnp.stack([third[1], third[0...  13.1 us
    unnamed x7, local copies, waits for them, and re-layouts  11.3 us
    all_to_all x1, blocking collectives, per_device(): lax.all_to_all(summed, 'ta', split_axis=3, concat_axis=1, tiled=True)  10.3 us
  transfers between devices with their start and end apart: 1, of which 1 were waited for; matrix products, arithmetic and copies ran while one was open for 0% of the time, Pallas kernels for 0%

commit v1 on v0

v1 whole, which is shorter than its diff:
```python
import functools
import math

import jax
import jax.numpy as jnp
from jax import lax
from jax.experimental import pallas as pl
from jax.experimental.pallas import tpu as pltpu
from jax.sharding import PartitionSpec as P

LY = 16
LZ = 16
UNROLL = 4
F32 = jnp.float32
BF16 = jnp.bfloat16


def phase_rows(position, momenta, first_site, site_count, extent_x):
    site = first_site + lax.broadcasted_iota(jnp.int32, (1, site_count), 1)
    coords = (site // (LY * LZ), site // LZ % LY, site % LZ)
    turns = 0.0
    for axis, extent in enumerate((extent_x, LY, LZ)):
        steps = momenta[:, axis : axis + 1] * (coords[axis] - position[axis])
        part = steps & (extent - 1) if extent & (extent - 1) == 0 else steps % extent
        turns = turns + part.astype(F32) / extent
    angle = (2.0 * math.pi) * turns
    return jnp.cos(angle).astype(BF16).astype(F32), jnp.sin(angle).astype(BF16).astype(F32)


def compute_kernel(
    extent_x, scale, prop_ref, rows_ref, sign_ref, site_ref, mom_ref, out_ref,
    field, left, right, total, select,
):
    src_count, time_count, _, width, _, site_count = prop_ref.shape
    terms = rows_ref.shape[0]
    moms = mom_ref.shape[0]
    pad = field.shape[2]
    group = max(1, 16 // moms)
    first_site = lax.axis_index("sa") * site_count
    first_source = lax.axis_index("src") * src_count

    field[...] = jnp.zeros_like(field)
    spot = lax.broadcasted_iota(jnp.int32, select.shape, 0)
    column = lax.broadcasted_iota(jnp.int32, select.shape, 1)
    inner = spot % pad
    keep = (column == spot // pad * width + inner) & (inner < width)
    select[...] = jnp.where(keep, 1.0, 0.0).astype(BF16)

    def slab(source, time, cos, sin):
        for part in range(2):
            for row in range(width):
                field[part, row, 0:width, :] = prop_ref[source, time, part, row].astype(F32)

        @pl.loop(0, width)
        def _(row):
            for i in range(0, width, group):
                reals, imags = [], []
                for one in range(i, i + group):
                    re = field[0, row, one : one + 1, :]
                    im = field[1, row, one : one + 1, :]
                    reals.append(cos * re + sin * im)
                    imags.append(cos * im - sin * re)
                re = jnp.concatenate(reals, axis=0).astype(BF16)
                im = jnp.concatenate(imags, axis=0)
                upper = pl.ds(i * moms, group * moms)
                lower = pl.ds((width + i) * moms, group * moms)
                left[row, upper, 0:site_count] = re
                left[row, upper, site_count:] = (-im).astype(BF16)
                left[row, lower, 0:site_count] = im.astype(BF16)
                left[row, lower, site_count:] = re

        total[...] = jnp.zeros_like(total)

        @pl.loop(0, terms // UNROLL)
        def _(step):
            added = None
            for u in range(UNROLL):
                term = step * UNROLL + u
                weight = (2 * sign_ref[term] - 1).astype(F32)
                second = rows_ref[term, 1]
                third = rows_ref[term, 2]
                re = weight * field[0, third]
                im = weight * field[1, third]
                for j in range(width):
                    a = field[0, second, j : j + 1, :]
                    b = field[1, second, j : j + 1, :]
                    lines = pl.ds(j * pad, pad)
                    right[u, lines, 0:site_count] = (a * re - b * im).astype(BF16)
                    right[u, lines, site_count:] = (a * im + b * re).astype(BF16)
                product = lax.dot_general(
                    left[rows_ref[term, 0]], right[u], (((1,), (1,)), ((), ())),
                    preferred_element_type=F32,
                )
                added = product if added is None else added + product
            total[...] += added

        value = total[...] * scale
        high = value.astype(BF16)
        rest = value - high.astype(F32)
        middle = rest.astype(BF16)
        low = (rest - middle.astype(F32)).astype(BF16)
        dense = sum(
            jnp.dot(piece, select[...], preferred_element_type=F32)
            for piece in (low, middle, high)
        )
        for o in range(2):
            pieces = [
                dense[(o * width + i) * moms : (o * width + i + 1) * moms, :]
                for i in range(width)
            ]
            out_ref[source, time, o] = jnp.concatenate(pieces, axis=1)

    for source in range(src_count):
        position = [site_ref[first_source + source, axis] for axis in range(3)]
        cos, sin = phase_rows(position, mom_ref[...], first_site, site_count, extent_x)

        @pl.loop(0, time_count)
        def _(time):
            slab(source, time, cos, sin)


def partial_blocks(prop, eps_rows, eps_sign, source_sites, momenta):
    src_count, time_count, _, width, _, site_count = prop.shape
    sites_total = site_count * lax.axis_size("sa")
    extent_x = sites_total // (LY * LZ)
    scale = 1.0 / math.sqrt(4.0 * eps_rows.shape[0] * sites_total)
    moms = momenta.shape[0]
    pad = -(-width // 16) * 16
    vmem = pl.BlockSpec(memory_space=pltpu.VMEM)
    smem = pl.BlockSpec(memory_space=pltpu.SMEM)
    return pl.pallas_call(
        functools.partial(compute_kernel, extent_x, scale),
        out_shape=jax.ShapeDtypeStruct((src_count, time_count, 2, moms, width**3), F32),
        in_specs=[vmem, smem, smem, smem, vmem],
        out_specs=vmem,
        scratch_shapes=[
            pltpu.VMEM((2, width, pad, site_count), F32),
            pltpu.VMEM((width, 2 * width * moms, 2 * site_count), BF16),
            pltpu.VMEM((UNROLL, width * pad, 2 * site_count), BF16),
            pltpu.VMEM((2 * width * moms, width * pad), F32),
            pltpu.VMEM((width * pad, width * width), BF16),
        ],
        compiler_params=pltpu.CompilerParams(vmem_limit_bytes=48 * 1024 * 1024),
        name="blocks",
    )(prop, eps_rows, eps_sign, source_sites, momenta)


def per_device(prop, eps_rows, eps_sign, source_sites, momenta):
    ta, sa = lax.axis_size("ta"), lax.axis_size("sa")
    value = partial_blocks(prop, eps_rows, eps_sign, source_sites, momenta)
    src_count, time_count, _, moms, comps = value.shape
    value = value.reshape(src_count, time_count, 2, ta, moms // ta, sa, comps // sa)
    value = value.transpose(3, 5, 0, 1, 2, 4, 6).reshape(
        ta * sa, src_count, time_count, 2, moms // ta, comps // sa
    )
    value = lax.all_to_all(value, ("ta", "sa"), split_axis=0, concat_axis=0, tiled=True)
    value = value.reshape((ta, sa) + value.shape[1:]).sum(axis=1)
    value = value.transpose(1, 0, 2, 3, 4, 5).reshape(
        src_count, ta * time_count, 2, moms // ta, comps // sa
    )
    return lax.all_gather(value, "src", axis=0, tiled=True)


def solution(mesh):
    return jax.shard_map(
        per_device,
        mesh=mesh,
        in_specs=(P(("cfg", "src"), "ta", None, None, None, "sa"), P(), P(), P("cfg", None), P()),
        out_specs=P("cfg", None, None, "ta", "sa"),
        check_vma=False,
    )
```

time: 325 us -> 28.2 us (0.09)
  local copies, waits for them, and re-layouts: 174 us -> 3.04 us
  matrix products: 86.5 us -> 0 us
  waiting for transfers between devices: 21.5 us -> 0 us
  other arithmetic: 15.3 us -> 0.09 us
  between operations: 13.5 us -> 0.06 us
  Pallas kernels: 0 us -> 7.27 us
  blocking collectives: 12.3 us -> 17.5 us
    dot_general x4 -> x0, matrix products: 86.5 us -> none  [the longest x2 82.4 us: contract(): jnp.einsum('ceijx,oceLx->oijLx', pair, mixer, preferred_element_type=jnp....]
    another operation x4 -> x1, local copies, waits for them, and re-layouts: 81.1 us -> 0.01 us  [per_device(): value.transpose(1, 0, 2, 3, 4, 5)]
    convert_element_type x2 -> x0, local copies, waits for them, and re-layouts: 58.5 us -> none  [contract(): block.astype(jnp.bfloat16)]
    unnamed x2 -> x0, waiting for transfers between devices: 21.5 us -> none
    unnamed x7 -> x9, local copies, waits for them, and re-layouts: 11.3 us -> 1.9 us
    gather x6 -> x0, local copies, waits for them, and re-layouts: 8.66 us -> none  [the longest x2 4.1 us: contract(): third = jnp.take(slab, rows[:, 2], axis=1)]
    pallas_call x0 -> x1, Pallas kernels: none -> 7.27 us  [partial_blocks(): pl.pallas_call(functools.partial(compute_kernel, extent_x, scale), out_sh...]
    all_to_all x1, blocking collectives: 10.3 us -> 15.5 us  [per_device(): lax.all_to_all(value, ('ta', 'sa'), split_axis=0, concat_axis=0, tiled=True)]
  transfers between devices with their start and end apart: 1 -> 0, of which waited for: 1 -> 0; matrix products, arithmetic and copies ran while one was open for 0% -> 0% of each run, Pallas kernels for 0% -> 0%
where the time goes in v1:
time: 28.2 us; the launch traced here: 27.9 us
  blocking collectives  17.5 us (62%)
  Pallas kernels  7.27 us (26%)
  local copies, waits for them, and re-layouts  3.04 us (11%)
    all_to_all x1, blocking collectives, per_device(): lax.all_to_all(value, ('ta', 'sa'), split_axis=0, concat_axis=0, tiled=True)  15.5 us
    pallas_call x1, Pallas kernels, partial_blocks(): pl.pallas_call(functools.partial(compute_kernel, extent_x, scale), out_sh...  7.27 us
    all_gather x1, blocking collectives, per_device(): return lax.all_gather(value, 'src', axis=0, tiled=True)  1.97 us
    unnamed x9, local copies, waits for them, and re-layouts  1.9 us
    all_gather x1, local copies, waits for them, and re-layouts, per_device(): return lax.all_gather(value, 'src', axis=0, tiled=True)  0.81 us

profile of v1, /device:TPU:0, one launch (start us, length us, event | category | flops | bytes accessed | tf_op | source)
XLA Modules:
  0.0 27.9 jit_solution(13477970192631775109)
XLA Ops:
  0.0 0.0 copy-start.2
  0.0 0.8 %copy.21.mom_ref = s32[8,3]{1,0:T(8,128)S(1)} copy(s32[8,3]{0,1:T(4,128)} %param.9) | data formatting | bytes 192 | tf_op args[4]
  0.8 0.0 copy-done.2
  0.8 0.1 copy.20.rows_ref
  0.9 0.0 copy-start
  0.9 0.0 copy-start.1
  0.9 1.0 %copy.19.prop_ref = bf16[1,2,2,12,12,256]{5,4,3,2,1,0:T(8,128)(2,1)S(1)} copy(bf16[1,2,2,12,12,256]{5,2,4,3,1,0:T(2,128)(2,1)} %param.5) | data formatting | bytes 589824 | tf_op args[0]
  1.9 0.0 copy-done
  1.9 0.0 copy-done.1
  1.9 7.3 %blocks.1 = f32[1,2,2,8,1728]{4,3,2,1,0:T(8,128)S(1)} custom-call(bf16[1,2,2,12,12,256]{5,4,3,2,1,0:T(8,128)(2,1)S(1)} %copy.19.prop_ref, s32[24,3]{1,0:T(8,128)S(1)} %copy.20.rows_ref, s32[24]{0:T(128)S(1)} %copy-done.1, s32[2,3]{1,0:T(2,128)S(1)} %copy-done, s32[8,3]{1,0:T(8,128)S(1)} %copy.21.mom_ref), custom_call_target="tpu_custom_call" | custom-call | tf_op jit(solution)/shard_map/blocks/pallas_call | solution.py:131
  9.2 0.2 reshape.11
  9.4 0.1 copy.22
  9.5 15.5 %all_to_all.5 = f32[8,1,2,2,2,864]{5,4,3,2,1,0:T(2,128)S(1)} all-to-all(f32[8,1,2,2,2,864]{5,4,3,2,1,0:T(2,128)S(1)} %bitcast.11), channel_id=1, replica_groups=mesh['cfg'=2,'ta'=4,'sa'=2,'src'=2] {'ta','sa'}, dimensions={0} | all-to-all | bytes 442368 | tf_op jit(solution)/shard_map/all_to_all | solution.py:156
  25.1 0.1 bitcast_reduce_fusion
  25.2 2.0 %all_gather.3 = f32[2,8,2,2,864]{4,1,3,2,0:T(8,128)S(1)} all-gather(f32[1,8,2,2,864]{4,1,3,2,0:T(8,128)S(1)} %copy.24), channel_id=1, replica_groups=mesh['cfg'=2,'ta'=4,'sa'=2,'src'=2] {'src'}, dimensions={0}, use_global_device_ids=true | all-gather | bytes 331776 | tf_op jit(solution)/shard_map/all_gather | solution.py:161
  27.1 0.8 %copy.25 = f32[2,8,2,2,864]{4,3,2,1,0:T(2,128)} copy(f32[2,8,2,2,864]{4,1,3,2,0:T(8,128)S(1)} %all_gather.3) | data formatting | bytes 442368 | tf_op jit(solution)/shard_map/all_gather | solution.py:161
  (1 shorter events, 0.0 us)
Async XLA Ops:
  0.0 0.8 %copy-start.2 = (s32[24,3]{0,1:T(4,128)S(1)}, s32[24,3]{0,1:T(4,128)}, u32[]{:S(2)}) copy-start(s32[24,3]{0,1:T(4,128)} %param.6) | copy-start | bytes 868
  0.9 1.0 %copy-start = (s32[2,3]{1,0:T(2,128)S(1)}, s32[2,3]{1,0:T(2,128)}, u32[]{:S(2)}) copy-start(s32[2,3]{1,0:T(2,128)} %site_ref.1) | copy-start | bytes 76
  0.9 1.1 %copy-start.1 = (s32[24]{0:T(128)S(1)}, s32[24]{0:T(128)}, u32[]{:S(2)}) copy-start(s32[24]{0:T(128)} %sign_ref.1) | copy-start | bytes 292

commit v2 on v1

--- a/solution.py
+++ b/solution.py
@@ -38,6 +38,7 @@
     group = max(1, 16 // moms)
     first_site = lax.axis_index("sa") * site_count
     first_source = lax.axis_index("src") * src_count
+    sa_size, ta_size = out_ref.shape[:2]
 
     field[...] = jnp.zeros_like(field)
     spot = lax.broadcasted_iota(jnp.int32, select.shape, 0)
@@ -103,34 +104,43 @@
             jnp.dot(piece, select[...], preferred_element_type=F32)
             for piece in (low, middle, high)
         )
+        share = width // sa_size
+        each = moms // ta_size
         for o in range(2):
-            pieces = [
-                dense[(o * width + i) * moms : (o * width + i + 1) * moms, :]
-                for i in range(width)
-            ]
-            out_ref[source, time, o] = jnp.concatenate(pieces, axis=1)
+            line = ((source * time_count + time) * 2 + o) * each
+            for piece in range(sa_size):
+                lines = [
+                    dense[(o * width + i) * moms : (o * width + i + 1) * moms, :]
+                    for i in range(piece * share, (piece + 1) * share)
+                ]
+                lines = jnp.concatenate(lines, axis=1)
+                for owner in range(ta_size):
+                    out_ref[piece, owner, line : line + each, :] = lines[
+                        owner * each : (owner + 1) * each
+                    ]
 
     for source in range(src_count):
         position = [site_ref[first_source + source, axis] for axis in range(3)]
         cos, sin = phase_rows(position, mom_ref[...], first_site, site_count, extent_x)
 
-        @pl.loop(0, time_count)
-        def _(time):
+        for time in range(time_count):
             slab(source, time, cos, sin)
 
 
 def partial_blocks(prop, eps_rows, eps_sign, source_sites, momenta):
     src_count, time_count, _, width, _, site_count = prop.shape
-    sites_total = site_count * lax.axis_size("sa")
+    sa, ta = lax.axis_size("sa"), lax.axis_size("ta")
+    sites_total = site_count * sa
     extent_x = sites_total // (LY * LZ)
     scale = 1.0 / math.sqrt(4.0 * eps_rows.shape[0] * sites_total)
     moms = momenta.shape[0]
+    rows = src_count * time_count * 2 * moms // ta
     pad = -(-width // 16) * 16
     vmem = pl.BlockSpec(memory_space=pltpu.VMEM)
     smem = pl.BlockSpec(memory_space=pltpu.SMEM)
     return pl.pallas_call(
         functools.partial(compute_kernel, extent_x, scale),
-        out_shape=jax.ShapeDtypeStruct((src_count, time_count, 2, moms, width**3), F32),
+        out_shape=jax.ShapeDtypeStruct((sa, ta, rows, width**3 // sa), F32),
         in_specs=[vmem, smem, smem, smem, vmem],
         out_specs=vmem,
         scratch_shapes=[
@@ -145,20 +155,100 @@
     )(prop, eps_rows, eps_sign, source_sites, momenta)
 
 
+def exchange_kernel(part_ref, out_ref, landed, summed, done, send_x, recv_x, send_z, recv_z, send_c, recv_c):
+    sa, ta = part_ref.shape[:2]
+    src = done.shape[0]
+    me_sa, me_ta, me_src = (lax.axis_index(name) for name in ("sa", "ta", "src"))
+
+    def send(source, target, sems, device):
+        copy = pltpu.make_async_remote_copy(
+            src_ref=source, dst_ref=target, send_sem=sems[0], recv_sem=sems[1],
+            device_id=device, device_id_type=pl.DeviceIdType.MESH,
+        )
+        copy.start()
+        return copy
+
+    barrier = pltpu.get_barrier_semaphore()
+    peers = [{"sa": lax.rem(me_sa + d, sa)} for d in range(1, sa)]
+    peers += [{"ta": lax.rem(me_ta + d, ta)} for d in range(1, ta)]
+    peers += [{"src": lax.rem(me_src + d, src)} for d in range(1, src)]
+    for peer in peers:
+        pl.semaphore_signal(barrier, inc=1, device_id=peer, device_id_type=pl.DeviceIdType.MESH)
+    pl.semaphore_wait(barrier, len(peers))
+
+    order = list(range(1, ta)) + [0]
+    owners = {d: lax.rem(me_ta + d, ta) for d in order}
+    over_x = {}
+    for d in order:
+        for e in range(1, sa):
+            target = lax.rem(me_sa + e, sa)
+            over_x[d, e] = send(
+                part_ref.at[target, owners[d]], landed.at[e - 1, d],
+                (send_x.at[e - 1, d], recv_x.at[e - 1, d]), {"sa": target},
+            )
+
+    over_z = {}
+    for d in order:
+        value = part_ref[me_sa, owners[d]]
+        for e in range(1, sa):
+            over_x[d, e].wait_recv()
+            value = value + landed[e - 1, d]
+        if d == 0:
+            done[me_src, me_ta] = value
+        else:
+            summed[d - 1] = value
+            over_z[d] = send(
+                summed.at[d - 1], done.at[me_src, me_ta],
+                (send_z.at[d - 1], recv_z.at[d - 1]), {"ta": owners[d]},
+            )
+
+    over_c = {}
+    for d in [0] + order[:-1]:
+        origin = lax.rem(me_ta - d + ta, ta)
+        if d:
+            over_z[d].wait_recv()
+        for e in range(1, src):
+            over_c[d, e] = send(
+                done.at[me_src, origin], done.at[me_src, origin],
+                (send_c.at[e - 1, d], recv_c.at[e - 1, d]),
+                {"src": lax.rem(me_src + e, src)},
+            )
+    for copy in over_c.values():
+        copy.wait_recv()
+    for copies in (over_x, over_z, over_c):
+        for copy in copies.values():
+            copy.wait_send()
+    out_ref[...] = done[...]
+
+
+def exchange(part):
+    sa, ta, rows, comps = part.shape
+    src = lax.axis_size("src")
+    vmem = pl.BlockSpec(memory_space=pltpu.VMEM)
+    pair = lambda *shape: [pltpu.SemaphoreType.DMA(shape)] * 2
+    return pl.pallas_call(
+        exchange_kernel,
+        out_shape=jax.ShapeDtypeStruct((src, ta, rows, comps), F32),
+        in_specs=[vmem],
+        out_specs=vmem,
+        scratch_shapes=[
+            pltpu.VMEM((sa - 1, ta, rows, comps), F32),
+            pltpu.VMEM((ta - 1, rows, comps), F32),
+            pltpu.VMEM((src, ta, rows, comps), F32),
+            *pair(sa - 1, ta), *pair(ta - 1), *pair(src - 1, ta),
+        ],
+        compiler_params=pltpu.CompilerParams(collective_id=0, has_side_effects=True),
+        name="exchange",
+    )(part)
+
+
 def per_device(prop, eps_rows, eps_sign, source_sites, momenta):
-    ta, sa = lax.axis_size("ta"), lax.axis_size("sa")
-    value = partial_blocks(prop, eps_rows, eps_sign, source_sites, momenta)
-    src_count, time_count, _, moms, comps = value.shape
-    value = value.reshape(src_count, time_count, 2, ta, moms // ta, sa, comps // sa)
-    value = value.transpose(3, 5, 0, 1, 2, 4, 6).reshape(
-        ta * sa, src_count, time_count, 2, moms // ta, comps // sa
-    )
-    value = lax.all_to_all(value, ("ta", "sa"), split_axis=0, concat_axis=0, tiled=True)
-    value = value.reshape((ta, sa) + value.shape[1:]).sum(axis=1)
-    value = value.transpose(1, 0, 2, 3, 4, 5).reshape(
-        src_count, ta * time_count, 2, moms // ta, comps // sa
-    )
-    return lax.all_gather(value, "src", axis=0, tiled=True)
+    src_count, time_count = prop.shape[:2]
+    done = exchange(partial_blocks(prop, eps_rows, eps_sign, source_sites, momenta))
+    src, ta, rows, comps = done.shape
+    done = done.reshape(src, ta, src_count, time_count, 2, -1, comps)
+    done = done.transpose(0, 2, 1, 3, 4, 5, 6)
+    return done.reshape(src * src_count, ta * time_count, 2, -1, comps)
 
 
 def solution(mesh):

time: 28.2 us -> 26.2 us (0.929)
  blocking collectives: 17.5 us -> 0 us
  Pallas kernels: 7.27 us -> 21.6 us
  local copies, waits for them, and re-layouts: 3.04 us -> 4.34 us
    all_to_all x1 -> x0, blocking collectives: 15.5 us -> none  [per_device(): lax.all_to_all(value, ('ta', 'sa'), split_axis=0, concat_axis=0, tiled=True)]
    pallas_call x0 -> x1, Pallas kernels: none -> 14.5 us  [exchange(): pl.pallas_call(exchange_kernel, out_shape=jax.ShapeDtypeStruct((src, ta,...]
    all_gather x1 -> x0, blocking collectives: 1.97 us -> none  [per_device(): return lax.all_gather(value, 'src', axis=0, tiled=True)]
    another operation x1, local copies, waits for them, and re-layouts: 0.01 us -> 1.76 us  [per_device(): return done.reshape(src * src_count, ta * time_count, 2, -1, comps)]
    all_gather x1 -> x0, local copies, waits for them, and re-layouts: 0.81 us -> none  [per_device(): return lax.all_gather(value, 'src', axis=0, tiled=True)]
    unnamed x9 -> x11, local copies, waits for them, and re-layouts: 1.9 us -> 2.58 us
    reshape x2 -> x0, local copies, waits for them, and re-layouts: 0.33 us -> none  [per_device(): value.reshape(src_count, time_count, 2, ta, moms // ta, sa, comps // sa)]
where the time goes in v2:
time: 26.2 us; the launch traced here: 26 us
  Pallas kernels  21.6 us (82%)
  local copies, waits for them, and re-layouts  4.34 us (17%)
    pallas_call x1, Pallas kernels, exchange(): pl.pallas_call(exchange_kernel, out_shape=jax.ShapeDtypeStruct((src, ta,...  14.5 us
    pallas_call x1, Pallas kernels, partial_blocks(): pl.pallas_call(functools.partial(compute_kernel, extent_x, scale), out_sh...  7.15 us
    unnamed x11, local copies, waits for them, and re-layouts  2.58 us
    another operation x1, local copies, waits for them, and re-layouts, per_device(): return done.reshape(src * src_count, ta * time_count, 2, -1, comps)  1.76 us

profile of v2, /device:TPU:0, one launch (start us, length us, event | category | flops | bytes accessed | tf_op | source)
XLA Modules:
  0.0 26.0 jit_solution(1856444773835125077)
XLA Ops:
  0.0 0.0 copy-start.3
  0.0 0.8 %copy.8.mom_ref = s32[8,3]{1,0:T(8,128)S(1)} copy(s32[8,3]{0,1:T(4,128)} %param.9) | data formatting | bytes 192 | tf_op args[4]
  0.8 0.0 copy-done.3
  0.8 0.1 copy.7.rows_ref
  0.9 0.0 copy-start.1
  0.9 0.0 copy-start.2
  0.9 1.0 %copy.6.prop_ref = bf16[1,2,2,12,12,256]{5,4,3,2,1,0:T(8,128)(2,1)S(1)} copy(bf16[1,2,2,12,12,256]{5,2,4,3,1,0:T(2,128)(2,1)} %param.5) | data formatting | bytes 589824 | tf_op args[0]
  1.9 0.0 copy-done.1
  1.9 0.0 copy-done.2
  1.9 7.2 %blocks.1.part_ref = f32[2,4,8,864]{3,2,1,0:T(8,128)S(1)} custom-call(bf16[1,2,2,12,12,256]{5,4,3,2,1,0:T(8,128)(2,1)S(1)} %copy.6.prop_ref, s32[24,3]{1,0:T(8,128)S(1)} %copy.7.rows_ref, s32[24]{0:T(128)S(1)} %copy-done.2, s32[2,3]{1,0:T(2,128)S(1)} %copy-done.1, s32[8,3]{1,0:T(8,128)S(1)} %copy.8.mom_ref), custom_call_target="tpu_custom_call" | custom-call | tf_op jit(solution)/shard_map/blocks/pallas_call | solution.py:141
  9.1 0.0 copy-start
  9.1 0.7 %copy-done = f32[2,4,8,864]{3,2,1,0:T(8,128)} copy-done((f32[2,4,8,864]{3,2,1,0:T(8,128)}, f32[2,4,8,864]{3,2,1,0:T(8,128)S(1)}, u32[]{:S(2)}) %copy-start) | copy-done | bytes 221208
  9.8 14.5 %exchange.1 = f32[2,4,8,864]{3,2,1,0:T(8,128)} custom-call(f32[2,4,8,864]{3,2,1,0:T(8,128)} %copy-done), custom_call_target="tpu_custom_call" | custom-call | tf_op jit(solution)/shard_map/exchange/pallas_call | solution.py:229
  24.2 1.8 %reshape_transpose_reshape.3 = f32[2,8,2,2,864]{4,3,2,1,0:T(2,128)} reshape(f32[2,4,8,864]{3,2,1,0:T(8,128)} %exchange.1) | data formatting | bytes 442368 | tf_op jit(solution)/shard_map/reshape;transpose;reshape | solution.py:251
Async XLA Ops:
  0.0 0.8 %copy-start.3 = (s32[24,3]{0,1:T(4,128)S(1)}, s32[24,3]{0,1:T(4,128)}, u32[]{:S(2)}) copy-start(s32[24,3]{0,1:T(4,128)} %param.6) | copy-start | bytes 868
  0.9 1.0 %copy-start.1 = (s32[2,3]{1,0:T(2,128)S(1)}, s32[2,3]{1,0:T(2,128)}, u32[]{:S(2)}) copy-start(s32[2,3]{1,0:T(2,128)} %site_ref.1) | copy-start | bytes 76
  0.9 1.1 %copy-start.2 = (s32[24]{0:T(128)S(1)}, s32[24]{0:T(128)}, u32[]{:S(2)}) copy-start(s32[24]{0:T(128)} %sign_ref.1) | copy-start | bytes 292
  9.1 0.7 %copy-start = (f32[2,4,8,864]{3,2,1,0:T(8,128)}, f32[2,4,8,864]{3,2,1,0:T(8,128)S(1)}, u32[]{:S(2)}) copy-start(f32[2,4,8,864]{3,2,1,0:T(8,128)S(1)} %blocks.1.part_ref) | copy-start | bytes 663556

commit v3 on v1

--- a/solution.py
+++ b/solution.py
@@ -17,27 +17,42 @@
 
 def phase_rows(position, momenta, first_site, site_count, extent_x):
     site = first_site + lax.broadcasted_iota(jnp.int32, (1, site_count), 1)
+    line = lax.broadcasted_iota(jnp.int32, (momenta.shape[1], site_count), 0)
     coords = (site // (LY * LZ), site // LZ % LY, site % LZ)
     turns = 0.0
     for axis, extent in enumerate((extent_x, LY, LZ)):
-        steps = momenta[:, axis : axis + 1] * (coords[axis] - position[axis])
+        factor = jnp.zeros_like(line)
+        for mom in range(momenta.shape[1]):
+            factor = jnp.where(line == mom, momenta[axis, mom], factor)
+        steps = factor * (coords[axis] - position[axis])
         part = steps & (extent - 1) if extent & (extent - 1) == 0 else steps % extent
         turns = turns + part.astype(F32) / extent
     angle = (2.0 * math.pi) * turns
     return jnp.cos(angle).astype(BF16).astype(F32), jnp.sin(angle).astype(BF16).astype(F32)
 
 
-def compute_kernel(
+def blocks_kernel(
     extent_x, scale, prop_ref, rows_ref, sign_ref, site_ref, mom_ref, out_ref,
-    field, left, right, total, select,
+    field, left, right, total, select, part_ref, landed, summed, done,
+    send_x, recv_x, send_z, recv_z, send_c, recv_c,
 ):
     src_count, time_count, _, width, _, site_count = prop_ref.shape
-    terms = rows_ref.shape[0]
-    moms = mom_ref.shape[0]
+    terms = rows_ref.shape[1]
+    moms = mom_ref.shape[1]
     pad = field.shape[2]
     group = max(1, 16 // moms)
     first_site = lax.axis_index("sa") * site_count
     first_source = lax.axis_index("src") * src_count
+    slabs, sa, ta = part_ref.shape[:3]
+    src = done.shape[0]
+    me_sa, me_ta, me_src = (lax.axis_index(name) for name in ("sa", "ta", "src"))
+
+    barrier = pltpu.get_barrier_semaphore()
+    peers = [{"sa": lax.rem(me_sa + d, sa)} for d in range(1, sa)]
+    peers += [{"ta": lax.rem(me_ta + d, ta)} for d in range(1, ta)]
+    peers += [{"src": lax.rem(me_src + d, src)} for d in range(1, src)]
+    for peer in peers:
+        pl.semaphore_signal(barrier, inc=1, device_id=peer, device_id_type=pl.DeviceIdType.MESH)
 
     field[...] = jnp.zeros_like(field)
     spot = lax.broadcasted_iota(jnp.int32, select.shape, 0)
@@ -77,8 +92,8 @@
             for u in range(UNROLL):
                 term = step * UNROLL + u
                 weight = (2 * sign_ref[term] - 1).astype(F32)
-                second = rows_ref[term, 1]
-                third = rows_ref[term, 2]
+                second = rows_ref[1, term]
+                third = rows_ref[2, term]
                 re = weight * field[0, third]
                 im = weight * field[1, third]
                 for j in range(width):
@@ -88,7 +103,7 @@
                     right[u, lines, 0:site_count] = (a * re - b * im).astype(BF16)
                     right[u, lines, site_count:] = (a * im + b * re).astype(BF16)
                 product = lax.dot_general(
-                    left[rows_ref[term, 0]], right[u], (((1,), (1,)), ((), ())),
+                    left[rows_ref[0, term]], right[u], (((1,), (1,)), ((), ())),
                     preferred_element_type=F32,
                 )
                 added = product if added is None else added + product
@@ -103,35 +118,99 @@
             jnp.dot(piece, select[...], preferred_element_type=F32)
             for piece in (low, middle, high)
         )
+        share = width // sa
+        each = moms // ta
         for o in range(2):
-            pieces = [
-                dense[(o * width + i) * moms : (o * width + i + 1) * moms, :]
-                for i in range(width)
-            ]
-            out_ref[source, time, o] = jnp.concatenate(pieces, axis=1)
+            for piece in range(sa):
+                lines = [
+                    dense[(o * width + i) * moms : (o * width + i + 1) * moms, :]
+                    for i in range(piece * share, (piece + 1) * share)
+                ]
+                lines = jnp.concatenate(lines, axis=1)
+                for owner in range(ta):
+                    part_ref[source * time_count + time, piece, owner, o] = lines[
+                        owner * each : (owner + 1) * each
+                    ]
+
+    def send(source, target, sems, device):
+        copy = pltpu.make_async_remote_copy(
+            src_ref=source, dst_ref=target, send_sem=sems[0], recv_sem=sems[1],
+            device_id=device, device_id_type=pl.DeviceIdType.MESH,
+        )
+        copy.start()
+        return copy
+
+    order = list(range(1, ta)) + [0]
+    owners = {d: lax.rem(me_ta + d, ta) for d in order}
+    over_x, over_z, over_c = {}, {}, {}
 
     for source in range(src_count):
         position = [site_ref[first_source + source, axis] for axis in range(3)]
-        cos, sin = phase_rows(position, mom_ref[...], first_site, site_count, extent_x)
-
-        @pl.loop(0, time_count)
-        def _(time):
+        cos, sin = phase_rows(position, mom_ref, first_site, site_count, extent_x)
+
+        for time in range(time_count):
             slab(source, time, cos, sin)
-
-
-def partial_blocks(prop, eps_rows, eps_sign, source_sites, momenta):
+            at = source * time_count + time
+            if at == 0:
+                pl.semaphore_wait(barrier, len(peers))
+            for d in order:
+                for e in range(1, sa):
+                    target = lax.rem(me_sa + e, sa)
+                    over_x[at, d, e] = send(
+                        part_ref.at[at, target, owners[d]], landed.at[e - 1, at, d],
+                        (send_x.at[e - 1, at, d], recv_x.at[e - 1, at, d]), {"sa": target},
+                    )
+
+    for at in range(slabs):
+        for d in order:
+            value = part_ref[at, me_sa, owners[d]]
+            for e in range(1, sa):
+                over_x[at, d, e].wait_recv()
+                value = value + landed[e - 1, at, d]
+            if d == 0:
+                done[me_src, me_ta, at] = value
+            else:
+                summed[d - 1, at] = value
+                over_z[at, d] = send(
+                    summed.at[d - 1, at], done.at[me_src, me_ta, at],
+                    (send_z.at[d - 1, at], recv_z.at[d - 1, at]), {"ta": owners[d]},
+                )
+
+    for at in range(slabs):
+        for d in [0] + order[:-1]:
+            origin = lax.rem(me_ta - d + ta, ta)
+            if d:
+                over_z[at, d].wait_recv()
+            for e in range(1, src):
+                over_c[at, d, e] = send(
+                    done.at[me_src, origin, at], done.at[me_src, origin, at],
+                    (send_c.at[e - 1, at, d], recv_c.at[e - 1, at, d]),
+                    {"src": lax.rem(me_src + e, src)},
+                )
+    for copy in over_c.values():
+        copy.wait_recv()
+    for copies in (over_x, over_z, over_c):
+        for copy in copies.values():
+            copy.wait_send()
+    out_ref[...] = done[...]
+
+
+def per_device(prop, eps_rows, eps_sign, source_sites, momenta):
     src_count, time_count, _, width, _, site_count = prop.shape
-    sites_total = site_count * lax.axis_size("sa")
+    sa, ta, src = (lax.axis_size(name) for name in ("sa", "ta", "src"))
+    sites_total = site_count * sa
     extent_x = sites_total // (LY * LZ)
     scale = 1.0 / math.sqrt(4.0 * eps_rows.shape[0] * sites_total)
     moms = momenta.shape[0]
+    each, comps, slabs = moms // ta, width**3 // sa, src_count * time_count
     pad = -(-width // 16) * 16
     vmem = pl.BlockSpec(memory_space=pltpu.VMEM)
     smem = pl.BlockSpec(memory_space=pltpu.SMEM)
-    return pl.pallas_call(
-        functools.partial(compute_kernel, extent_x, scale),
-        out_shape=jax.ShapeDtypeStruct((src_count, time_count, 2, moms, width**3), F32),
-        in_specs=[vmem, smem, smem, smem, vmem],
+    pair = lambda *shape: [pltpu.SemaphoreType.DMA(shape)] * 2
+    done = pl.pallas_call(
+        functools.partial(blocks_kernel, extent_x, scale),
+        out_shape=jax.ShapeDtypeStruct((src, ta, slabs, 2, each, comps), F32),
+        in_specs=[vmem, smem, smem, smem, smem],
         out_specs=vmem,
         scratch_shapes=[
             pltpu.VMEM((2, width, pad, site_count), F32),
@@ -139,26 +218,20 @@
             pltpu.VMEM((UNROLL, width * pad, 2 * site_count), BF16),
             pltpu.VMEM((2 * width * moms, width * pad), F32),
             pltpu.VMEM((width * pad, width * width), BF16),
+            pltpu.VMEM((slabs, sa, ta, 2, each, comps), F32),
+            pltpu.VMEM((sa - 1, slabs, ta, 2, each, comps), F32),
+            pltpu.VMEM((ta - 1, slabs, 2, each, comps), F32),
+            pltpu.VMEM((src, ta, slabs, 2, each, comps), F32),
+            *pair(sa - 1, slabs, ta), *pair(ta - 1, slabs), *pair(src - 1, slabs, ta),
         ],
-        compiler_params=pltpu.CompilerParams(vmem_limit_bytes=48 * 1024 * 1024),
+        compiler_params=pltpu.CompilerParams(
+            vmem_limit_bytes=48 * 1024 * 1024, collective_id=0, has_side_effects=True
+        ),
         name="blocks",
-    )(prop, eps_rows, eps_sign, source_sites, momenta)
-
-
-def per_device(prop, eps_rows, eps_sign, source_sites, momenta):
-    ta, sa = lax.axis_size("ta"), lax.axis_size("sa")
-    value = partial_blocks(prop, eps_rows, eps_sign, source_sites, momenta)
-    src_count, time_count, _, moms, comps = value.shape
-    value = value.reshape(src_count, time_count, 2, ta, moms // ta, sa, comps // sa)
-    value = value.transpose(3, 5, 0, 1, 2, 4, 6).reshape(
-        ta * sa, src_count, time_count, 2, moms // ta, comps // sa
-    )
-    value = lax.all_to_all(value, ("ta", "sa"), split_axis=0, concat_axis=0, tiled=True)
-    value = value.reshape((ta, sa) + value.shape[1:]).sum(axis=1)
-    value = value.transpose(1, 0, 2, 3, 4, 5).reshape(
-        src_count, ta * time_count, 2, moms // ta, comps // sa
-    )
-    return lax.all_gather(value, "src", axis=0, tiled=True)
+    )(prop, eps_rows.T, eps_sign, source_sites, momenta.T)
+    done = done.reshape(src, ta, src_count, time_count, 2, each, comps)
+    done = done.transpose(0, 2, 1, 3, 4, 5, 6)
+    return done.reshape(src * src_count, ta * time_count, 2, each, comps)
 
 
 def solution(mesh):

time: 28.2 us -> 20.5 us (0.73)
  blocking collectives: 17.5 us -> 0 us
  Pallas kernels: 7.27 us -> 18.5 us
  local copies, waits for them, and re-layouts: 3.04 us -> 1.77 us
    all_to_all x1 -> x0, blocking collectives: 15.5 us -> none  [per_device(): lax.all_to_all(value, ('ta', 'sa'), split_axis=0, concat_axis=0, tiled=True)]
    pallas_call x1, Pallas kernels: 7.27 us -> 18.5 us  [per_device(): pl.pallas_call(functools.partial(blocks_kernel, extent_x, scale), out_sha...]
    all_gather x1 -> x0, blocking collectives: 1.97 us -> none  [per_device(): return lax.all_gather(value, 'src', axis=0, tiled=True)]
    all_gather x1 -> x0, local copies, waits for them, and re-layouts: 0.81 us -> none  [per_device(): return lax.all_gather(value, 'src', axis=0, tiled=True)]
    reshape x2 -> x0, local copies, waits for them, and re-layouts: 0.33 us -> none  [per_device(): value.reshape(src_count, time_count, 2, ta, moms // ta, sa, comps // sa)]
    unnamed x9 -> x10, local copies, waits for them, and re-layouts: 1.9 us -> 1.77 us
where the time goes in v3:
time: 20.5 us; the launch traced here: 20.3 us
  Pallas kernels  18.5 us (90%)
  local copies, waits for them, and re-layouts  1.77 us (9%)
    pallas_call x1, Pallas kernels, per_device(): pl.pallas_call(functools.partial(blocks_kernel, extent_x, scale), out_sha...  18.5 us
    unnamed x10, local copies, waits for them, and re-layouts  1.77 us

profile of v3, /device:TPU:0, one launch (start us, length us, event | category | flops | bytes accessed | tf_op | source)
XLA Modules:
  0.0 20.3 jit_solution(14668313655272223509)
XLA Ops:
  0.0 0.0 copy-start
  0.0 0.0 copy-start.1
  0.0 0.0 copy-start.2
  0.0 0.0 copy-start.3
  0.0 1.1 %copy.6.prop_ref = bf16[1,2,2,12,12,256]{5,4,3,2,1,0:T(8,128)(2,1)S(1)} copy(bf16[1,2,2,12,12,256]{5,2,4,3,1,0:T(2,128)(2,1)} %param.5) | data formatting | bytes 589824 | tf_op args[0]
  1.1 0.0 copy-done
  1.1 0.0 copy-done.1
  1.1 0.0 copy-done.2
  1.1 0.0 copy-done.3
  1.1 18.5 %blocks.1 = f32[2,4,2,2,2,864]{5,4,3,2,1,0:T(2,128)S(1)} custom-call(bf16[1,2,2,12,12,256]{5,4,3,2,1,0:T(8,128)(2,1)S(1)} %copy.6.prop_ref, s32[3,24]{1,0:T(4,128)S(1)} %bitcast.4, s32[24]{0:T(128)S(1)} %copy-done.3, s32[2,3]{1,0:T(2,128)S(1)} %copy-done.2, s32[3,8]{1,0:T(4,128)S(1)} %bitcast.5), custom_call_target="tpu_custom_call" | custom-call | tf_op jit(solution)/shard_map/blocks/pallas_call | solution.py:210
  19.6 0.7 %copy.8 = f32[2,8,2,2,864]{4,3,2,1,0:T(2,128)} copy(f32[2,8,2,2,864]{4,3,2,1,0:T(2,128)S(1)} %bitcast.3) | data formatting | bytes 442368
Async XLA Ops:
  0.0 1.1 %copy-start = (s32[24,3]{0,1:T(4,128)S(1)}, s32[24,3]{0,1:T(4,128)}, u32[]{:S(2)}) copy-start(s32[24,3]{0,1:T(4,128)} %param.6) | copy-start | bytes 868
  0.0 1.1 %copy-start.1 = (s32[8,3]{0,1:T(4,128)S(1)}, s32[8,3]{0,1:T(4,128)}, u32[]{:S(2)}) copy-start(s32[8,3]{0,1:T(4,128)} %param.9) | copy-start | bytes 292
  0.0 1.1 %copy-start.2 = (s32[2,3]{1,0:T(2,128)S(1)}, s32[2,3]{1,0:T(2,128)}, u32[]{:S(2)}) copy-start(s32[2,3]{1,0:T(2,128)} %site_ref.1) | copy-start | bytes 76
  0.0 1.1 %copy-start.3 = (s32[24]{0:T(128)S(1)}, s32[24]{0:T(128)}, u32[]{:S(2)}) copy-start(s32[24]{0:T(128)} %sign_ref.1) | copy-start | bytes 292
